TPU v7x, 256 devices: a 4x2x16 block of a 4x16x16 slice. The times are simulated.
256 devices in a mesh: groups: 2 (over y), mp: 16 (over z), expert: 4 (over x), dp: 2 (over core).
Axes of the slice: x: 4, y: 2, z: 16, core: 2. Of those that a mesh axis runs over, the one named last changes fastest.
The devices are a block of a 4x16x16 slice.
Arguments:
- hidden_in: bfloat16 [1024, 4096], P(('groups', 'expert', 'dp'), 'mp'), parts along dimension 0, may hold values from -6 to 6
- norm_gain: bfloat16 [2, 4096], P(None, 'mp'), may hold values from 0.25 to 1.75
- expert_ids: int32 [2, 1024, 2], P(None, ('groups', 'expert', 'dp')), parts along dimension 1, may hold values from 0 to 3, all different within a row; in each aligned block of 64 rows (0 to 63, 64 to 127, ..., all dimensions but the last counted through in order) at most 64 rows name the same one
- gate_counts: int32 [2, 1024, 2], P(None, ('groups', 'expert', 'dp')), parts along dimension 1, may hold values from 8 to 15
- exit_layer: int32 [1024], P(('groups', 'expert', 'dp')), parts along dimension 0, may hold values from 1 to 2
- w_gate: bfloat16 [2, 4, 7168, 4096], P(None, 'expert', ('mp', 'dp')), may hold values from -0.09375 to 0.09375
- w_up: bfloat16 [2, 4, 7168, 4096], P(None, 'expert', ('mp', 'dp')), may hold values from -0.09375 to 0.09375
- w_down: bfloat16 [2, 4, 7168, 4096], P(None, 'expert', ('mp', 'dp')), may hold values from -0.0625 to 0.0625
Outputs:
- hidden_out: bfloat16 [1024, 4096], P(('groups', 'expert', 'dp'), 'mp'), parts along dimension 0
There are 2 independent parts, one for each index of `groups`. A program takes and returns all parts, laid end to end along the dimension named above; an argument that names none is the same for every part. Nothing has to cross between parts.
Inputs may be any that keep to these rules, and one draw needn't show every extreme that they name: `expert_ids`: A token's two ids in a layer differ. In the rows of one device in one layer (aligned blocks of 64 rows, layer by layer) some expert may be named by all 64 rows.
All inputs are finite; a program needn't handle non-finite values.
Results may differ from a plain program's by a relative error of at most 0.014.
Values may be sent and summed in bfloat16 or wider, within the bound.
A program may use at most 128 MiB of HBM per device.

v0:
```python
import jax
import jax.numpy as jnp
from jax import lax
from jax.sharding import PartitionSpec as P

LAYERS = 2
norm_floor = 0.1


def rows_first(arrays, axis, dims):
    turned = [jnp.moveaxis(a, dim, 0) for a, dim in zip(arrays, dims)]
    both = jnp.concatenate([t.reshape(len(t), -1) for t in turned], axis=1)
    whole, at, outs = (lax.all_gather(both, axis, axis=0, tiled=True), 0, [])
    for t, dim in zip(turned, dims):
        section = whole[:, at : at + t[0].size].reshape(-1, *t.shape[1:])
        outs.append(jnp.moveaxis(section, 0, dim))
        at += t[0].size
    return tuple(outs)


def side_by_side(arrays, axis, dim, along):
    ends, at = ([], 0)
    for a in arrays[:-1]:
        at += a.shape[along]
        ends.append(at)
    both = jnp.concatenate(arrays, axis=along)
    return tuple(jnp.split(lax.all_gather(both, axis, axis=dim, tiled=True), ends, axis=along))


def body(hidden_in, norm_gain, expert_ids, gate_counts, exit_layer, w_gate, w_up, w_down):
    experts = lax.axis_size("expert")
    shards = lax.axis_size("mp")
    tok_rows, slice_width = hidden_in.shape
    full_width = slice_width * shards
    contract = (((1,), (1,)), ((), ()))
    expert_range = jnp.arange(experts, dtype=jnp.int32)
    slot_range = jnp.arange(tok_rows, dtype=jnp.int32)
    current = hidden_in
    for layer_idx in range(LAYERS):
        counts = gate_counts[layer_idx].astype(jnp.float32)
        gate_share = counts / jnp.sum(counts, axis=1, keepdims=True)
        active = exit_layer > layer_idx
        matched = (expert_ids[layer_idx][:, :, None] == expert_range[None, None, :]) & active[
            :, None, None
        ]
        chosen = jnp.sum(matched.astype(jnp.int32), axis=1)
        weight_te = jnp.sum(jnp.where(matched, gate_share[:, :, None], jnp.float32(0.0)), axis=1)
        slot_rank = jnp.cumsum(chosen, axis=0) - chosen
        place_mask = (slot_rank.T[:, None, :] == slot_range[None, :, None]) & (
            chosen.T[:, None, :] > 0
        )
        place_bf = place_mask.astype(jnp.bfloat16)
        current_f32 = current.astype(jnp.float32)
        whole_rows, whole_gain = rows_first((current, norm_gain[layer_idx]), "mp", (1, 0))
        whole_f32 = whole_rows.astype(jnp.float32)
        sum_squares = jnp.sum(whole_f32 * whole_f32, axis=1)
        inv_rms = lax.rsqrt(sum_squares / full_width + norm_floor)
        normed = (whole_f32 * inv_rms[:, None] * whole_gain.astype(jnp.float32)[None, :]).astype(
            jnp.bfloat16
        )
        outgoing = jnp.einsum(
            "ect,td->ecd", place_bf, normed, preferred_element_type=jnp.float32
        ).astype(jnp.bfloat16)
        incoming = lax.all_to_all(outgoing, "expert", split_axis=0, concat_axis=0, tiled=True)
        inputs = incoming.reshape(experts * tok_rows, full_width)
        gate_rows, up_rows, down_rows = side_by_side(
            (w_gate[layer_idx, 0], w_up[layer_idx, 0], w_down[layer_idx, 0]), "dp", 0, 1
        )
        gate_val = lax.dot_general(inputs, gate_rows, contract, preferred_element_type=jnp.float32)
        up_val = lax.dot_general(inputs, up_rows, contract, preferred_element_type=jnp.float32)
        hidden = (jax.nn.silu(gate_val) * up_val).astype(jnp.bfloat16)
        partial_value = jnp.dot(hidden, down_rows, preferred_element_type=jnp.float32)
        summed = lax.psum_scatter(
            partial_value.astype(jnp.bfloat16), "mp", scatter_dimension=1, tiled=True
        )
        returned = lax.all_to_all(
            summed.reshape(experts, tok_rows, slice_width),
            "expert",
            split_axis=0,
            concat_axis=0,
            tiled=True,
        )
        place_weight = place_mask.astype(jnp.float32) * weight_te.T[:, None, :]
        update = jnp.einsum("ect,ecd->td", place_weight, returned.astype(jnp.float32))
        current = (current_f32 + update).astype(jnp.bfloat16)
    return current


def solution(mesh):
    in_specs = (
        P(("groups", "expert", "dp"), "mp"),
        P(None, "mp"),
        P(None, ("groups", "expert", "dp"), None),
        P(None, ("groups", "expert", "dp"), None),
        P(("groups", "expert", "dp")),
        P(None, "expert", ("mp", "dp"), None),
        P(None, "expert", ("mp", "dp"), None),
        P(None, "expert", ("mp", "dp"), None),
    )
    out_specs = P(("groups", "expert", "dp"), "mp")
    return jax.shard_map(body, mesh=mesh, in_specs=in_specs, out_specs=out_specs, check_vma=False)
```

profile of v0, /device:TPU:40, one launch (start us, length us, event | category | flops | bytes accessed | tf_op | source)
XLA Modules:
  0.0 336.3 jit_solution(16841984590572916138)
XLA Ops:
  6.6 2.5 slice_bitcast_fusion.5
  9.1 0.6 copy-done
  9.7 1.1 copy-done.1
  10.8 2.8 slice_bitcast_fusion.3
  13.6 5.6 %pad_maximum_fusion = bf16[224,12288]{1,0:T(8,128)(2,1)} fusion(bf16[224,4096]{1,0:T(8,128)(2,1)S(1)} %get-tuple-element.11, bf16[224,4096]{1,0:T(8,128)(2,1)S(1)} %get-tuple-element.22, bf16[224,4096]{1,0:T(8,128)(2,1)S(1)} %get-tuple-element.7), kind=kLoop, calls=%fused_computation | loop fusion | flops 16515072 | bytes 11010048 | tf_op jit(solution)/shard_map/concatenate | solution.py:26
  20.2 51.8 %all_gather.12 = bf16[4096,65]{0,1:T(8,128)(2,1)S(1)} all-gather(bf16[256,65]{0,1:T(8,128)(2,1)S(1)} %pad_maximum_fusion.2), channel_id=1, replica_groups=mesh['groups'=2,'mp'=16,'expert'=4,'dp'=2] {'mp'}, dimensions={0}, use_global_device_ids=true | all-gather | bytes 565760 | tf_op jit(solution)/shard_map/all_gather | solution.py:13
  72.2 0.9 convolution_convert_fusion.3
  73.1 23.9 %all_to_all.20 = bf16[4,64,4096]{2,1,0:T(8,128)(2,1)} all-to-all(bf16[4,64,4096]{2,1,0:T(8,128)(2,1)S(1)} %convolution_convert_fusion.3), channel_id=1, replica_groups=mesh['groups'=2,'mp'=16,'expert'=4,'dp'=2] {'expert'}, dimensions={0} | all-to-all | bytes 4194304 | tf_op jit(solution)/shard_map/all_to_all | solution.py:64
  97.0 3.8 %fusion.8 = f32[256,448]{0,1:T(8,128)S(1)} fusion(bf16[256,4096]{1,0:T(8,128)(2,1)} %bitcast.68, bf16[448,12288]{1,0:T(8,128)(2,1)} %all-gather.3.cloned.1.call-done), kind=kOutput, calls=%fused_computation.14 | convolution fusion | flops 939524096 | bytes 6225920 | tf_op jit(solution)/shard_map/dot_general | solution.py:69
  100.8 9.4 %convolution_convert_fusion.2 = bf16[256,4096]{1,0:T(8,128)(2,1)} fusion(bf16[448,12288]{1,0:T(8,128)(2,1)} %all-gather.3.cloned.1.call-done, bf16[256,4096]{1,0:T(8,128)(2,1)} %bitcast.69, f32[256,448]{0,1:T(8,128)S(1)} %fusion.8), kind=kOutput, calls=%fused_computation.4 | convolution fusion | flops 1880784896 | bytes 11993088 | tf_op jit(solution)/shard_map/dot_general | solution.py:72
  110.3 4.9 %pad_maximum_fusion.1 = bf16[224,12288]{1,0:T(8,128)(2,1)} fusion(bf16[224,4096]{1,0:T(8,128)(2,1)} %get-tuple-element.12, bf16[224,4096]{1,0:T(8,128)(2,1)} %get-tuple-element.21, bf16[224,4096]{1,0:T(8,128)(2,1)S(1)} %get-tuple-element.8), kind=kLoop, calls=%fused_computation.1 | loop fusion | flops 16515072 | bytes 11010048 | tf_op jit(solution)/shard_map/concatenate | solution.py:26
  115.9 57.0 %reduce-scatter.3.cloned.1.call-done = bf16[256,256]{1,0:T(8,128)(2,1)} async-done(((bf16[256,4096]{1,0:T(8,128)(2,1)}), bf16[256,256]{1,0:T(8,128)(2,1)}) %reduce-scatter.3.cloned.1.call-update) | async-done | bytes 131088 | tf_op jit(solution)/shard_map/reduce_scatter | solution.py:73
  172.9 4.3 %all-to-all-start.1 = ((bf16[4,64,256]{2,1,0:T(8,128)(2,1)}), bf16[4,64,256]{2,1,0:T(8,128)(2,1)S(1)}, u32[]{:S(2)}, u32[]{:S(2)}) async-start(bf16[4,64,256]{2,1,0:T(8,128)(2,1)} %bitcast.70), calls=%async_computation.2 | async-start | bytes 262144 | tf_op jit(solution)/shard_map/all_to_all | solution.py:76
  177.3 6.0 %all-to-all-done.1 = bf16[4,64,256]{2,1,0:T(8,128)(2,1)S(1)} async-done(((bf16[4,64,256]{2,1,0:T(8,128)(2,1)}), bf16[4,64,256]{2,1,0:T(8,128)(2,1)S(1)}, u32[]{:S(2)}, u32[]{:S(2)}) %all-to-all-start.1) | async-done | bytes 131104 | tf_op jit(solution)/shard_map/all_to_all | solution.py:76
  183.5 30.7 %all_gather.14 = bf16[4096,65]{0,1:T(8,128)(2,1)S(1)} all-gather(bf16[256,65]{0,1:T(8,128)(2,1)S(1)} %pad_maximum_fusion.3), channel_id=1, replica_groups=mesh['groups'=2,'mp'=16,'expert'=4,'dp'=2] {'mp'}, dimensions={0}, use_global_device_ids=true | all-gather | bytes 565760 | tf_op jit(solution)/shard_map/all_gather | solution.py:13
  214.5 2.2 convolution_convert_fusion.1
  216.7 3.7 %all-to-all-start.2 = ((bf16[4,64,4096]{2,1,0:T(8,128)(2,1)}), bf16[4,64,4096]{2,1,0:T(8,128)(2,1)S(1)}, u32[]{:S(2)}, u32[]{:S(2)}) async-start(bf16[4,64,4096]{2,1,0:T(8,128)(2,1)} %convolution_convert_fusion.1), calls=%async_computation.3 | async-start | bytes 4194304 | tf_op jit(solution)/shard_map/all_to_all | solution.py:64
  220.7 16.1 %all-to-all-done.2 = bf16[4,64,4096]{2,1,0:T(8,128)(2,1)S(1)} async-done(((bf16[4,64,4096]{2,1,0:T(8,128)(2,1)}), bf16[4,64,4096]{2,1,0:T(8,128)(2,1)S(1)}, u32[]{:S(2)}, u32[]{:S(2)}) %all-to-all-start.2) | async-done | bytes 2097184 | tf_op jit(solution)/shard_map/all_to_all | solution.py:64
  236.8 3.2 fusion.3
  240.0 8.8 %convolution_convert_fusion = bf16[256,4096]{1,0:T(8,128)(2,1)} fusion(bf16[448,12288]{1,0:T(8,128)(2,1)} %all-gather.5.cloned.1.call-done, bf16[256,4096]{1,0:T(8,128)(2,1)S(1)} %bitcast.67, f32[256,448]{0,1:T(8,128)S(1)} %fusion.3), kind=kOutput, calls=%fused_computation.2 | convolution fusion | flops 1880784896 | bytes 11993088 | tf_op jit(solution)/shard_map/dot_general | solution.py:72
  248.9 69.8 %reduce-scatter.5.cloned.1.call-done = bf16[256,256]{1,0:T(8,128)(2,1)} async-done(((bf16[256,4096]{1,0:T(8,128)(2,1)}), bf16[256,256]{1,0:T(8,128)(2,1)}) %reduce-scatter.5.cloned.1.call-update) | async-done | bytes 131088 | tf_op jit(solution)/shard_map/reduce_scatter | solution.py:73
  318.7 4.2 %all-to-all-start.3 = ((bf16[4,64,256]{2,1,0:T(8,128)(2,1)}), bf16[4,64,256]{2,1,0:T(8,128)(2,1)S(1)}, u32[]{:S(2)}, u32[]{:S(2)}) async-start(bf16[4,64,256]{2,1,0:T(8,128)(2,1)} %bitcast.71), calls=%async_computation.5 | async-start | bytes 262144 | tf_op jit(solution)/shard_map/all_to_all | solution.py:76
  322.9 6.0 %all-to-all-done.3 = bf16[4,64,256]{2,1,0:T(8,128)(2,1)S(1)} async-done(((bf16[4,64,256]{2,1,0:T(8,128)(2,1)}), bf16[4,64,256]{2,1,0:T(8,128)(2,1)S(1)}, u32[]{:S(2)}, u32[]{:S(2)}) %all-to-all-start.3) | async-done | bytes 131104 | tf_op jit(solution)/shard_map/all_to_all | solution.py:76
  328.9 0.9 fusion.28
  (50 shorter events, 2.9 us)
Async XLA Ops:
  6.5 90.4 %all-gather.3.cloned.1.call-start = ((), (), s32[]{:S(2)}) async-start(), calls=%async_computation.6 | async-start | bytes 16515072 | tf_op jit(solution)/shard_map/all_gather | solution.py:27
  6.6 3.1 copy-start
  6.6 4.3 %copy-start.1 = (bf16[2,1,224,4096]{3,2,1,0:T(8,128)(2,1)S(1)}, bf16[2,1,224,4096]{3,2,1,0:T(8,128)(2,1)}, u32[]{:S(2)}) copy-start(bf16[2,1,224,4096]{3,2,1,0:T(8,128)(2,1)} %param.14) | copy-start | bytes 11010052
  19.1 0.7 copy-start.6
  19.1 0.7 copy-start.5
  19.1 1.0 copy-start.4
  19.1 1.0 copy-start.2
  19.2 153.7 %reduce-scatter.3.cloned.1.call-start = ((), (), s32[]{:S(2)}) async-start(), calls=%async_computation.7 | async-start | bytes 2228224 | tf_op jit(solution)/shard_map/reduce_scatter | solution.py:73
  110.2 110.5 %all-gather.5.cloned.1.call-start = ((), (), s32[]{:S(2)}) async-start(), calls=%async_computation.8 | async-start | bytes 16515072 | tf_op jit(solution)/shard_map/all_gather | solution.py:27
  115.2 0.7 copy-start.3
  172.9 10.3 %all-to-all-start.1 = ((bf16[4,64,256]{2,1,0:T(8,128)(2,1)}), bf16[4,64,256]{2,1,0:T(8,128)(2,1)S(1)}, u32[]{:S(2)}, u32[]{:S(2)}) async-start(bf16[4,64,256]{2,1,0:T(8,128)(2,1)} %bitcast.70), calls=%async_computation.2 | async-start | bytes 262144 | tf_op jit(solution)/shard_map/all_to_all | solution.py:76
  216.7 20.1 %all-to-all-start.2 = ((bf16[4,64,4096]{2,1,0:T(8,128)(2,1)}), bf16[4,64,4096]{2,1,0:T(8,128)(2,1)S(1)}, u32[]{:S(2)}, u32[]{:S(2)}) async-start(bf16[4,64,4096]{2,1,0:T(8,128)(2,1)} %convolution_convert_fusion.1), calls=%async_computation.3 | async-start | bytes 4194304 | tf_op jit(solution)/shard_map/all_to_all | solution.py:64
  220.4 98.3 %reduce-scatter.5.cloned.1.call-start = ((), (), s32[]{:S(2)}) async-start(), calls=%async_computation.9 | async-start | bytes 2228224 | tf_op jit(solution)/shard_map/reduce_scatter | solution.py:73
  318.7 10.2 %all-to-all-start.3 = ((bf16[4,64,256]{2,1,0:T(8,128)(2,1)}), bf16[4,64,256]{2,1,0:T(8,128)(2,1)S(1)}, u32[]{:S(2)}, u32[]{:S(2)}) async-start(bf16[4,64,256]{2,1,0:T(8,128)(2,1)} %bitcast.71), calls=%async_computation.5 | async-start | bytes 262144 | tf_op jit(solution)/shard_map/all_to_all | solution.py:76
Sparse Core Ops, SparseCore 0:
  19.3 45.2 all-gather.2
  110.4 62.5 reduce-scatter.2
  174.8 29.9 all-gather.4
  249.0 69.6 reduce-scatter.4
where the time goes:
time: 337 us; the launch traced here: 336 us
  waiting for transfers between devices  155 us (46%)
  blocking collectives  106 us (31%)
  matrix products  29.4 us (9%)
  between operations  13.3 us (4%)
  starting transfers between devices  12.6 us (4%)
  other arithmetic  11.3 us (3%)
  local copies, waits for them, and re-layouts  8.24 us (2%)
    reduce_scatter x2, waiting for transfers between devices, body(): lax.psum_scatter(partial_value.astype(jnp.bfloat16), 'mp', scatter_dimens...  127 us
    all_gather x2, blocking collectives, rows_first(): whole, at, outs = (lax.all_gather(both, axis, axis=0, tiled=True), 0, [])  82.5 us
    all_to_all x1, blocking collectives, body(): lax.all_to_all(outgoing, 'expert', split_axis=0, concat_axis=0, tiled=True)  23.9 us
    dot_general x2, matrix products, body(): jnp.dot(hidden, down_rows, preferred_element_type=jnp.float32)  18.2 us
    all_to_all x1, waiting for transfers between devices, body(): lax.all_to_all(outgoing, 'expert', split_axis=0, concat_axis=0, tiled=True)  16.1 us
    all_to_all x2, waiting for transfers between devices, body(): lax.all_to_all(summed.reshape(experts, tok_rows, slice_width), 'expert',...  11.9 us
    concatenate x2, other arithmetic, side_by_side(): both = jnp.concatenate(arrays, axis=along)  10.5 us
    all_to_all x2, starting transfers between devices, body(): lax.all_to_all(summed.reshape(experts, tok_rows, slice_width), 'expert',...  8.52 us
  transfers between devices with their start and end apart: 7, of which 5 were waited for; matrix products, arithmetic and copies ran while one was open for 3% of the time, Pallas kernels for 0%

commit v1 on v0

--- a/solution.py
+++ b/solution.py
@@ -5,6 +5,18 @@
 
 LAYERS = 2
 norm_floor = 0.1
+
+
+def cut_along(x, dim, size):
+    lengths = x.shape
+    blocks = x.reshape(*lengths[:dim], size, lengths[dim] // size, *lengths[dim + 1 :])
+    return jnp.moveaxis(blocks, dim, 0)
+
+
+def joined_along(tiles, dim):
+    lengths = list(tiles.shape[1:])
+    lengths[dim] *= tiles.shape[0]
+    return jnp.moveaxis(tiles, 0, dim).reshape(lengths)
 
 
 def rows_first(arrays, axis, dims):
@@ -61,7 +73,14 @@
         outgoing = jnp.einsum(
             "ect,td->ecd", place_bf, normed, preferred_element_type=jnp.float32
         ).astype(jnp.bfloat16)
-        incoming = lax.all_to_all(outgoing, "expert", split_axis=0, concat_axis=0, tiled=True)
+        size, here = (lax.axis_size("expert"), lax.axis_index("expert"))
+        blocks = cut_along(outgoing, 0, size)
+        gathered = [blocks[here]]
+        for step in range(1, size):
+            sent = blocks[here ^ step]
+            gathered.append(lax.ppermute(sent, "expert", [(i, i ^ step) for i in range(size)]))
+        blocks = jnp.stack(gathered)[here ^ jnp.arange(size)]
+        incoming = joined_along(blocks, 0)
         inputs = incoming.reshape(experts * tok_rows, full_width)
         gate_rows, up_rows, down_rows = side_by_side(
             (w_gate[layer_idx, 0], w_up[layer_idx, 0], w_down[layer_idx, 0]), "dp", 0, 1

time: 337 us -> 339 us (level)
  blocking collectives: 106 us -> 82.3 us
  waiting for transfers between devices: 155 us -> 170 us
  local copies, waits for them, and re-layouts: 8.24 us -> 14.6 us
  starting transfers between devices: 12.6 us -> 18.4 us
    ppermute x0 -> x6, waiting for transfers between devices: none -> 32.6 us  [body(): lax.ppermute(sent, 'expert', [(i, i ^ step) for i in range(size)])]
    all_to_all x1 -> x0, blocking collectives: 23.9 us -> none  [body(): lax.all_to_all(outgoing, 'expert', split_axis=0, concat_axis=0, tiled=True)]
    all_to_all x1 -> x0, waiting for transfers between devices: 16.1 us -> none  [body(): lax.all_to_all(outgoing, 'expert', split_axis=0, concat_axis=0, tiled=True)]
    ppermute x0 -> x6, starting transfers between devices: none -> 9.64 us  [body(): lax.ppermute(sent, 'expert', [(i, i ^ step) for i in range(size)])]
    gather x0 -> x2, local copies, waits for them, and re-layouts: none -> 4.03 us  [body(): blocks = jnp.stack(gathered)[here ^ jnp.arange(size)]]
    all_to_all x1 -> x0, starting transfers between devices: 3.7 us -> none  [body(): lax.all_to_all(outgoing, 'expert', split_axis=0, concat_axis=0, tiled=True)]
  transfers between devices with their start and end apart: 7 -> 12, of which waited for: 5 -> 10; matrix products, arithmetic and copies ran while one was open for 3% -> 4% of each run, Pallas kernels for 0% -> 0%
where the time goes in v1:
time: 339 us
  waiting for transfers between devices  170 us (50%)
  blocking collectives  82.3 us (24%)
  matrix products  28.4 us (8%)
  starting transfers between devices  18.4 us (5%)
  local copies, waits for them, and re-layouts  14.6 us (4%)
  between operations  13.3 us (4%)
  other arithmetic  11.8 us (3%)
    reduce_scatter x2, waiting for transfers between devices, body(): lax.psum_scatter(partial_value.astype(jnp.bfloat16), 'mp', scatter_dimens...  125 us
    all_gather x2, blocking collectives, rows_first(): whole, at, outs = (lax.all_gather(both, axis, axis=0, tiled=True), 0, [])  82.3 us
    ppermute x6, waiting for transfers between devices, body(): lax.ppermute(sent, 'expert', [(i, i ^ step) for i in range(size)])  32.6 us
    dot_general x2, matrix products, body(): jnp.dot(hidden, down_rows, preferred_element_type=jnp.float32)  17.6 us
    all_to_all x2, waiting for transfers between devices, body(): lax.all_to_all(summed.reshape(experts, tok_rows, slice_width), 'expert',...  11.9 us
    concatenate x2, other arithmetic, side_by_side(): both = jnp.concatenate(arrays, axis=along)  10.5 us
    ppermute x6, starting transfers between devices, body(): lax.ppermute(sent, 'expert', [(i, i ^ step) for i in range(size)])  9.64 us
    all_to_all x2, starting transfers between devices, body(): lax.all_to_all(summed.reshape(experts, tok_rows, slice_width), 'expert',...  8.47 us
  transfers between devices with their start and end apart: 12, of which 10 were waited for; matrix products, arithmetic and copies ran while one was open for 4% of the time, Pallas kernels for 0%

profile of v1, /device:TPU:40, one launch (start us, length us, event | category | flops | bytes accessed | tf_op | source)
XLA Modules:
  0.0 339.0 jit_solution(2961642594299645470)
XLA Ops:
  6.6 3.9 %slice_bitcast_fusion.5 = (bf16[224,4096]{1,0:T(8,128)(2,1)S(1)}, bf16[224,4096]{1,0:T(8,128)(2,1)}) fusion(bf16[2,1,224,4096]{3,2,1,0:T(8,128)(2,1)} %param.13), kind=kLoop, calls=%fused_computation.25 | loop fusion | bytes 7340032 | tf_op jit(solution)/shard_map/squeeze | solution.py:86
  11.5 2.7 slice_bitcast_fusion.3
  14.2 5.6 %pad_maximum_fusion = bf16[224,12288]{1,0:T(8,128)(2,1)} fusion(bf16[224,4096]{1,0:T(8,128)(2,1)S(1)} %get-tuple-element.11, bf16[224,4096]{1,0:T(8,128)(2,1)S(1)} %get-tuple-element.30, bf16[224,4096]{1,0:T(8,128)(2,1)S(1)} %get-tuple-element.7), kind=kLoop, calls=%fused_computation.2 | loop fusion | flops 16515072 | bytes 11010048 | tf_op jit(solution)/shard_map/concatenate | solution.py:38
  20.8 51.8 %all_gather.12 = bf16[4096,65]{0,1:T(8,128)(2,1)S(1)} all-gather(bf16[256,65]{0,1:T(8,128)(2,1)S(1)} %pad_maximum_fusion.2), channel_id=1, replica_groups=mesh['groups'=2,'mp'=16,'expert'=4,'dp'=2] {'mp'}, dimensions={0}, use_global_device_ids=true | all-gather | bytes 565760 | tf_op jit(solution)/shard_map/all_gather | solution.py:25
  75.7 3.0 collective-permute-start.1
  78.8 7.7 %collective-permute-done = bf16[1,64,4096]{2,1,0:T(8,128)(2,1)S(1)} collective-permute-done((bf16[1,64,4096]{2,1,0:T(8,128)(2,1)S(1)}, bf16[1,64,4096]{2,1,0:T(8,128)(2,1)S(1)}, u32[]{:S(2)}, u32[]{:S(2)}) %collective-permute-start) | collective-permute-done | bytes 524320 | tf_op jit(solution)/shard_map/ppermute | solution.py:81
  86.5 8.3 %collective-permute-done.1 = bf16[1,64,4096]{2,1,0:T(8,128)(2,1)S(1)} collective-permute-done((bf16[1,64,4096]{2,1,0:T(8,128)(2,1)S(1)}, bf16[1,64,4096]{2,1,0:T(8,128)(2,1)S(1)}, u32[]{:S(2)}, u32[]{:S(2)}) %collective-permute-start.1) | collective-permute-done | bytes 524320 | tf_op jit(solution)/shard_map/ppermute | solution.py:81
  94.8 2.5 collective-permute-done.2
  99.6 4.0 %fusion.8 = f32[256,448]{0,1:T(8,128)S(1)} fusion(bf16[256,4096]{1,0:T(8,128)(2,1)} %bitcast.84, bf16[448,12288]{1,0:T(8,128)(2,1)} %all-gather.3.cloned.1.call-done), kind=kOutput, calls=%fused_computation.16 | convolution fusion | flops 939524096 | bytes 6225920 | tf_op jit(solution)/shard_map/dot_general | solution.py:88
  103.6 8.8 %convolution_convert_fusion.2 = bf16[256,4096]{1,0:T(8,128)(2,1)} fusion(bf16[448,12288]{1,0:T(8,128)(2,1)} %all-gather.3.cloned.1.call-done, bf16[256,4096]{1,0:T(8,128)(2,1)S(1)} %bitcast.85, f32[256,448]{0,1:T(8,128)S(1)} %fusion.8), kind=kOutput, calls=%fused_computation.6 | convolution fusion | flops 1880784896 | bytes 11993088 | tf_op jit(solution)/shard_map/dot_general | solution.py:91
  113.9 4.9 %pad_maximum_fusion.1 = bf16[224,12288]{1,0:T(8,128)(2,1)} fusion(bf16[224,4096]{1,0:T(8,128)(2,1)} %get-tuple-element.12, bf16[224,4096]{1,0:T(8,128)(2,1)} %get-tuple-element.29, bf16[224,4096]{1,0:T(8,128)(2,1)S(1)} %copy-done), kind=kLoop, calls=%fused_computation.3 | loop fusion | flops 16515072 | bytes 11010048 | tf_op jit(solution)/shard_map/concatenate | solution.py:38
  119.5 55.1 %reduce-scatter.3.cloned.1.call-done = bf16[256,256]{1,0:T(8,128)(2,1)} async-done(((bf16[256,4096]{1,0:T(8,128)(2,1)}), bf16[256,256]{1,0:T(8,128)(2,1)}) %reduce-scatter.3.cloned.1.call-update) | async-done | bytes 131088 | tf_op jit(solution)/shard_map/reduce_scatter | solution.py:92
  174.6 4.3 %all-to-all-start = ((bf16[4,64,256]{2,1,0:T(8,128)(2,1)}), bf16[4,64,256]{2,1,0:T(8,128)(2,1)S(1)}, u32[]{:S(2)}, u32[]{:S(2)}) async-start(bf16[4,64,256]{2,1,0:T(8,128)(2,1)} %bitcast.92), calls=%async_computation.1 | async-start | bytes 262144 | tf_op jit(solution)/shard_map/all_to_all | solution.py:95
  178.9 6.0 %all-to-all-done = bf16[4,64,256]{2,1,0:T(8,128)(2,1)S(1)} async-done(((bf16[4,64,256]{2,1,0:T(8,128)(2,1)}), bf16[4,64,256]{2,1,0:T(8,128)(2,1)S(1)}, u32[]{:S(2)}, u32[]{:S(2)}) %all-to-all-start) | async-done | bytes 131104 | tf_op jit(solution)/shard_map/all_to_all | solution.py:95
  185.2 30.5 %all_gather.14 = bf16[4096,65]{0,1:T(8,128)(2,1)S(1)} all-gather(bf16[256,65]{0,1:T(8,128)(2,1)S(1)} %pad_maximum_fusion.3), channel_id=1, replica_groups=mesh['groups'=2,'mp'=16,'expert'=4,'dp'=2] {'mp'}, dimensions={0}, use_global_device_ids=true | all-gather | bytes 565760 | tf_op jit(solution)/shard_map/all_gather | solution.py:25
  217.7 2.1 collective-permute-start.4
  221.8 4.5 %collective-permute-done.3 = bf16[1,64,4096]{2,1,0:T(8,128)(2,1)S(1)} collective-permute-done((bf16[1,64,4096]{2,1,0:T(8,128)(2,1)S(1)}, bf16[1,64,4096]{2,1,0:T(8,128)(2,1)S(1)}, u32[]{:S(2)}, u32[]{:S(2)}) %collective-permute-start.3) | collective-permute-done | bytes 524320 | tf_op jit(solution)/shard_map/ppermute | solution.py:81
  226.3 6.4 %collective-permute-done.4 = bf16[1,64,4096]{2,1,0:T(8,128)(2,1)S(1)} collective-permute-done((bf16[1,64,4096]{2,1,0:T(8,128)(2,1)S(1)}, bf16[1,64,4096]{2,1,0:T(8,128)(2,1)S(1)}, u32[]{:S(2)}, u32[]{:S(2)}) %collective-permute-start.4) | collective-permute-done | bytes 524320 | tf_op jit(solution)/shard_map/ppermute | solution.py:81
  232.7 3.1 collective-permute-done.5
  238.2 4.0 %fusion.3 = f32[256,448]{0,1:T(8,128)S(1)} fusion(bf16[256,4096]{1,0:T(8,128)(2,1)} %bitcast.82, bf16[448,12288]{1,0:T(8,128)(2,1)} %all-gather.5.cloned.1.call-done), kind=kOutput, calls=%fused_computation.11 | convolution fusion | flops 939524096 | bytes 6225920 | tf_op jit(solution)/shard_map/dot_general | solution.py:88
  242.1 8.8 %convolution_convert_fusion = bf16[256,4096]{1,0:T(8,128)(2,1)} fusion(bf16[448,12288]{1,0:T(8,128)(2,1)} %all-gather.5.cloned.1.call-done, bf16[256,4096]{1,0:T(8,128)(2,1)S(1)} %bitcast.83, f32[256,448]{0,1:T(8,128)S(1)} %fusion.3), kind=kOutput, calls=%fused_computation.4 | convolution fusion | flops 1880784896 | bytes 11993088 | tf_op jit(solution)/shard_map/dot_general | solution.py:91
  251.0 70.4 %reduce-scatter.5.cloned.1.call-done = bf16[256,256]{1,0:T(8,128)(2,1)} async-done(((bf16[256,4096]{1,0:T(8,128)(2,1)}), bf16[256,256]{1,0:T(8,128)(2,1)}) %reduce-scatter.5.cloned.1.call-update) | async-done | bytes 131088 | tf_op jit(solution)/shard_map/reduce_scatter | solution.py:92
  321.4 4.2 %all-to-all-start.1 = ((bf16[4,64,256]{2,1,0:T(8,128)(2,1)}), bf16[4,64,256]{2,1,0:T(8,128)(2,1)S(1)}, u32[]{:S(2)}, u32[]{:S(2)}) async-start(bf16[4,64,256]{2,1,0:T(8,128)(2,1)} %bitcast.93), calls=%async_computation.3 | async-start | bytes 262144 | tf_op jit(solution)/shard_map/all_to_all | solution.py:95
  325.5 6.0 %all-to-all-done.1 = bf16[4,64,256]{2,1,0:T(8,128)(2,1)S(1)} async-done(((bf16[4,64,256]{2,1,0:T(8,128)(2,1)}), bf16[4,64,256]{2,1,0:T(8,128)(2,1)S(1)}, u32[]{:S(2)}, u32[]{:S(2)}) %all-to-all-start.1) | async-done | bytes 131104 | tf_op jit(solution)/shard_map/all_to_all | solution.py:95
  (73 shorter events, 17.2 us)
Async XLA Ops:
  6.5 93.1 %all-gather.3.cloned.1.call-start = ((), (), s32[]{:S(2)}) async-start(), calls=%async_computation.4 | async-start | bytes 16515072 | tf_op jit(solution)/shard_map/all_gather | solution.py:39
  6.6 3.9 %copy-start.1 = (bf16[2,1,224,4096]{3,2,1,0:T(8,128)(2,1)S(1)}, bf16[2,1,224,4096]{3,2,1,0:T(8,128)(2,1)}, u32[]{:S(2)}) copy-start(bf16[2,1,224,4096]{3,2,1,0:T(8,128)(2,1)} %param.15) | copy-start | bytes 11010052
  6.6 4.9 %copy-start.2 = (bf16[2,1,224,4096]{3,2,1,0:T(8,128)(2,1)S(1)}, bf16[2,1,224,4096]{3,2,1,0:T(8,128)(2,1)}, u32[]{:S(2)}) copy-start(bf16[2,1,224,4096]{3,2,1,0:T(8,128)(2,1)} %param.14) | copy-start | bytes 11010052
  19.8 0.7 copy-start.9
  19.8 0.7 copy-start.8
  19.8 1.0 copy-start.7
  19.8 1.0 copy-start.5
  19.9 154.7 %reduce-scatter.3.cloned.1.call-start = ((), (), s32[]{:S(2)}) async-start(), calls=%async_computation.5 | async-start | bytes 2228224 | tf_op jit(solution)/shard_map/reduce_scatter | solution.py:92
  74.0 12.5 %collective-permute-start = (bf16[1,64,4096]{2,1,0:T(8,128)(2,1)S(1)}, bf16[1,64,4096]{2,1,0:T(8,128)(2,1)S(1)}, u32[]{:S(2)}, u32[]{:S(2)}) collective-permute-start(bf16[1,64,4096]{2,1,0:T(8,128)(2,1)S(1)} %get-tuple-element.20), channel_id=1, source_target_pairs={{0,2},{2,0},{4,6},{6,4},{1,3},{3,1},{5,7},{7,5},{8,10},{10,8},{12,... | collective-permute-start | bytes 1572872 | tf_op jit(solution)/shard_map/ppermute | solution.py:81
  75.7 19.1 %collective-permute-start.1 = (bf16[1,64,4096]{2,1,0:T(8,128)(2,1)S(1)}, bf16[1,64,4096]{2,1,0:T(8,128)(2,1)S(1)}, u32[]{:S(2)}, u32[]{:S(2)}) collective-permute-start(bf16[1,64,4096]{2,1,0:T(8,128)(2,1)S(1)} %get-tuple-element.19), channel_id=1, source_target_pairs={{0,4},{2,6},{4,0},{6,2},{1,5},{3,7},{5,1},{7,3},{8,12},{10,14},{12... | collective-permute-start | bytes 1572872 | tf_op jit(solution)/shard_map/ppermute | solution.py:81
  78.7 18.6 %collective-permute-start.2 = (bf16[1,64,4096]{2,1,0:T(8,128)(2,1)S(1)}, bf16[1,64,4096]{2,1,0:T(8,128)(2,1)S(1)}, u32[]{:S(2)}, u32[]{:S(2)}) collective-permute-start(bf16[1,64,4096]{2,1,0:T(8,128)(2,1)S(1)} %get-tuple-element.18), channel_id=1, source_target_pairs={{0,6},{2,4},{4,2},{6,0},{1,7},{3,5},{5,3},{7,1},{8,14},{10,12},{12... | collective-permute-start | bytes 1572872 | tf_op jit(solution)/shard_map/ppermute | solution.py:81
  99.6 4.0 %copy-start.4 = (bf16[4,64,4096]{2,1,0:T(8,128)(2,1)S(1)}, bf16[4,64,4096]{2,1,0:T(8,128)(2,1)}, u32[]{:S(2)}) copy-start(bf16[4,64,4096]{2,1,0:T(8,128)(2,1)} %gather_fusion) | copy-start | bytes 6291460
  112.4 1.5 copy-start
  112.4 125.7 %all-gather.5.cloned.1.call-start = ((), (), s32[]{:S(2)}) async-start(), calls=%async_computation.6 | async-start | bytes 16515072 | tf_op jit(solution)/shard_map/all_gather | solution.py:39
  118.8 0.7 copy-start.6
  174.6 10.3 %all-to-all-start = ((bf16[4,64,256]{2,1,0:T(8,128)(2,1)}), bf16[4,64,256]{2,1,0:T(8,128)(2,1)S(1)}, u32[]{:S(2)}, u32[]{:S(2)}) async-start(bf16[4,64,256]{2,1,0:T(8,128)(2,1)} %bitcast.92), calls=%async_computation.1 | async-start | bytes 262144 | tf_op jit(solution)/shard_map/all_to_all | solution.py:95
  178.9 142.5 %reduce-scatter.5.cloned.1.call-start = ((), (), s32[]{:S(2)}) async-start(), calls=%async_computation.7 | async-start | bytes 2228224 | tf_op jit(solution)/shard_map/reduce_scatter | solution.py:92
  217.0 9.3 %collective-permute-start.3 = (bf16[1,64,4096]{2,1,0:T(8,128)(2,1)S(1)}, bf16[1,64,4096]{2,1,0:T(8,128)(2,1)S(1)}, u32[]{:S(2)}, u32[]{:S(2)}) collective-permute-start(bf16[1,64,4096]{2,1,0:T(8,128)(2,1)S(1)} %get-tuple-element.16), channel_id=1, source_target_pairs={{0,2},{2,0},{4,6},{6,4},{1,3},{3,1},{5,7},{7,5},{8,10},{10,8},{12,... | collective-permute-start | bytes 1572872 | tf_op jit(solution)/shard_map/ppermute | solution.py:81
  217.7 15.0 %collective-permute-start.4 = (bf16[1,64,4096]{2,1,0:T(8,128)(2,1)S(1)}, bf16[1,64,4096]{2,1,0:T(8,128)(2,1)S(1)}, u32[]{:S(2)}, u32[]{:S(2)}) collective-permute-start(bf16[1,64,4096]{2,1,0:T(8,128)(2,1)S(1)} %get-tuple-element.15), channel_id=1, source_target_pairs={{0,4},{2,6},{4,0},{6,2},{1,5},{3,7},{5,1},{7,3},{8,12},{10,14},{12... | collective-permute-start | bytes 1572872 | tf_op jit(solution)/shard_map/ppermute | solution.py:81
  219.9 16.0 %collective-permute-start.5 = (bf16[1,64,4096]{2,1,0:T(8,128)(2,1)S(1)}, bf16[1,64,4096]{2,1,0:T(8,128)(2,1)S(1)}, u32[]{:S(2)}, u32[]{:S(2)}) collective-permute-start(bf16[1,64,4096]{2,1,0:T(8,128)(2,1)S(1)} %get-tuple-element.14), channel_id=1, source_target_pairs={{0,6},{2,4},{4,2},{6,0},{1,7},{3,5},{5,3},{7,1},{8,14},{10,12},{12... | collective-permute-start | bytes 1572872 | tf_op jit(solution)/shard_map/ppermute | solution.py:81
  238.2 4.0 %copy-start.3 = (bf16[4,64,4096]{2,1,0:T(8,128)(2,1)S(1)}, bf16[4,64,4096]{2,1,0:T(8,128)(2,1)}, u32[]{:S(2)}) copy-start(bf16[4,64,4096]{2,1,0:T(8,128)(2,1)} %gather_fusion.1) | copy-start | bytes 6291460
  321.4 10.1 %all-to-all-start.1 = ((bf16[4,64,256]{2,1,0:T(8,128)(2,1)}), bf16[4,64,256]{2,1,0:T(8,128)(2,1)S(1)}, u32[]{:S(2)}, u32[]{:S(2)}) async-start(bf16[4,64,256]{2,1,0:T(8,128)(2,1)} %bitcast.93), calls=%async_computation.3 | async-start | bytes 262144 | tf_op jit(solution)/shard_map/all_to_all | solution.py:95
Sparse Core Ops, SparseCore 0:
  20.0 45.2 all-gather.2
  112.6 61.9 reduce-scatter.2
  176.4 29.7 all-gather.4
  251.1 70.2 reduce-scatter.4
